TPU v7x, 512 devices: a whole 4x8x8 slice. The times are simulated.
512 devices in a mesh: seq: 32 (over z_hi, y, core), mp: 16 (over z_lo, x).
Axes of the slice: x: 4, y: 8, z: 8 (z_hi: 2, z_lo: 4; z = z_hi * 4 + z_lo), core: 2. Of those that a mesh axis runs over, the one named last changes fastest.
Arguments:
- inputs: bfloat16 [32768, 4096], P('seq', 'mp'), may hold values from -6 to 6
- conv_weight: bfloat16 [4, 4096], P(None, 'mp'), may hold values from -3 to 3
- conv_bias: bfloat16 [4096], P('mp'), may hold values from -3 to 3
- doc_start: int32 [32768], P('seq'), may hold values from 0 to 32767, as said below
- counts: int32 [32], P('seq'), may hold values from 341 to 1024
Outputs:
- gram: float32 [4096, 4096], P('seq', 'mp')
Inputs may be any that keep to these rules, and one draw needn't show every extreme that they name: doc_start is never above the token's own position, and for t > 0 either doc_start[t] == t or doc_start[t] == doc_start[t - 1]; doc_start[0] is 0.
All inputs are finite; a program needn't handle non-finite values.
Results may differ from a plain program's by a relative error of at most 0.0003.
Values may be sent and summed in bfloat16 or wider, within the bound.
No kernel may reach another device: no remote copies, remote signals or barrier semaphores. Data moves between devices by JAX's collectives and lax.ppermute only.
A program may use at most 64 MiB of HBM per device.

v0:
```python
import functools

import jax
import jax.numpy as jnp
import numpy as np
from jax import lax
from jax.experimental import pallas as pl
from jax.experimental.pallas import tpu as pltpu
from jax.sharding import Mesh
from jax.sharding import PartitionSpec as P


ZH, YW, YA, CORE, ZL, X = AXES = ("zh", "yw", "ya", "core", "zl", "x")
SIZES = (2, 2, 4, 2, 4, 4)
SEQ = (ZH, YW, YA, CORE)
CHIPS = (ZH, YW, YA)
TAU = (3, 2, 0, 1)
EARLY = ((0, "own"), (0, "far"), (2, "own"), (2, "far"))
LATE = ((1, "own"), (1, "far"), (1, "near"), (3, "own"), (3, "far"), (3, "near"), (0, "near"), (2, "near"))
HALF = 128
EXTRA = 8
PACK = 8
LEVELS = 32767.0
VMEM = pl.BlockSpec(memory_space=pltpu.VMEM)
SMEM = pl.BlockSpec(memory_space=pltpu.SMEM)


def delivery():
    def number(seq_chip, core, mp):
        return (seq_chip * 2 + core) * 16 + mp

    edges = []
    for seq_chip in range(16):
        for h in range(2):
            for mp in range(16):
                zeta, a = divmod(seq_chip, 4)
                z, x = divmod(mp, 4)
                row = 4 * z + a
                if zeta == z:
                    col, hc = 4 * z + x, (h if a >= x else 1 - h)
                elif zeta == z ^ 1:
                    col, hc = 4 * (z ^ 1) + x, (h if z % 2 else 1 - h)
                else:
                    col, hc = 4 * TAU[z] + x, (0 if zeta == z ^ 2 else 1)
                src = number(seq_chip, h, mp)
                if row == col:
                    continue
                edges.append((src, number(row, h, col), hc, 0))
                edges.append((src, number(col, hc, row), h, 1))
    by_src, by_dst = {}, {}
    for e, (s, d, _, _) in enumerate(edges):
        by_src.setdefault(s, []).append(e)
        by_dst.setdefault(d, []).append(e)
    colour = {}
    for first in range(len(edges)):
        e = first
        while e not in colour:
            colour[e] = 0
            s = edges[e][0]
            other = [k for k in by_src[s] if k != e][0]
            colour[other] = 1
            d = edges[other][1]
            e = [k for k in by_dst[d] if k != other][0]
    pairs = ([], [])
    table = np.zeros((512, 4), np.int32)
    for e, (s, d, half, turned) in enumerate(edges):
        k = colour[e]
        pairs[k].append((s, d))
        table[d, 2 * k] = turned
        if k == 0:
            table[d, 1] = half
    for mp in range(16):
        for h in range(2):
            own, other = number(mp, h, mp), number(mp, 1 - h, mp)
            pairs[1].append((own, other))
            table[own] = (0, h, 0, 1)
    return pairs, table


def around(x, axis, by):
    n = lax.axis_size(axis)
    return lax.ppermute(x, axis, [((i + by) % n, i) for i in range(n)])


def flipped(x, axis, bit=1):
    n = lax.axis_size(axis)
    return lax.ppermute(x, axis, [(i, i ^ bit) for i in range(n)])


def products(late, where_ref, *refs):
    x, z, core, count = where_ref[0], where_ref[1], where_ref[2], where_ref[3]
    keep, send = refs[-2:]
    rows = dict(zip((0, 2, 1, 3) if late else (0, 2), refs))
    cols = {"own": refs[0], "far": refs[4], "near": refs[5]} if late else {"own": refs[0], "far": refs[2]}
    dims = (((0,), (0,)), ((), ()))
    r = lax.broadcasted_iota(jnp.int32, (HALF, HALF), 0)
    c = lax.broadcasted_iota(jnp.int32, (HALF, HALF), 1)
    extra_row = lax.broadcasted_iota(jnp.int32, (EXTRA, HALF), 0)
    counted = jnp.where(extra_row == 1, count.astype(jnp.float32), 0.0)
    found = {}
    for o, kind in LATE if late else EARLY:
        a = lax.rem(x + o, 4)
        p = lax.dot_general(rows[o][...], cols[kind][...], dims, preferred_element_type=jnp.float32)
        p00, p01, p10, p11 = p[:HALF, :HALF], p[:HALF, HALF:], p[HALF:, :HALF], p[HALF:, HALF:]
        extra = counted
        if kind == "own":
            same = r <= c if o == 0 else a > x
            found[0, o] = jnp.where(same, p00, p01), jnp.where(same, p11, p10)
            if o == 0:
                middle = jnp.sum(jnp.where(r == c, p01, 0.0), axis=0, keepdims=True)
                extra = jnp.where(extra_row == 0, middle, counted)
        elif kind == "near":
            same = lax.rem(z, 2) == 1
            found[1, o] = jnp.where(same, p00, p01), jnp.where(same, p11, p10)
        else:
            found[2, o] = p00, p10
            found[3, o] = p01, p11
        for k in {"own": (0,), "near": (1,), "far": (2, 3)}[kind]:
            at = slots(late).index((k, o))
            q0, q1 = found[k, o]
            keep[at, :HALF] = jnp.where(core == 0, q0, q1)
            send[at, :HALF] = jnp.where(core == 0, q1, q0)
            keep[at, HALF:] = extra
            send[at, HALF:] = extra


def slots(late):
    kinds = {"own": (0,), "near": (1,), "far": (2, 3)}
    return [(k, o) for o, kind in (LATE if late else EARLY) for k in kinds[kind]]


def multiplied(late, where, *blocks):
    shape = jax.ShapeDtypeStruct((len(slots(late)), HALF + EXTRA, HALF), jnp.float32)
    return pl.pallas_call(
        functools.partial(products, late),
        out_shape=(shape, shape),
        in_specs=[SMEM] + [VMEM] * len(blocks),
        out_specs=(VMEM, VMEM),
        compiler_params=pltpu.CompilerParams(vmem_limit_bytes=16 << 20),
        cost_estimate=pl.CostEstimate(
            flops=(1 << 27) * len(LATE if late else EARLY), bytes_accessed=5 << 20, transcendentals=0
        ),
        name="products_late" if late else "products_early",
    )(where, *blocks)


def scale_of(code):
    return jnp.exp2(code * (1.0 / 256.0))


def encode(late, where_ref, keep, got, *refs):
    row = lax.broadcasted_iota(jnp.int32, (PACK, HALF), 0)
    out = refs[-1]
    for at, (k, o) in enumerate(slots(late)):
        v = keep[at, :HALF] + got[at, :HALF]
        extra = keep[at, HALF:] + got[at, HALF:]
        middle, count = extra[0:1], extra[1:2]
        most = jnp.maximum(jnp.max(jnp.abs(v), axis=0, keepdims=True), jnp.abs(middle))
        code = jnp.ceil(jnp.log2(jnp.maximum(most, 1e-37)) * 256.0)
        rate = LEVELS / scale_of(code)
        tail = jnp.where(row == 0, middle * rate, jnp.where(row == 1, code, jnp.where(row == 2, count, 0.0)))
        slot = place(where_ref, k, o) if late else at
        out[slot, :HALF] = whole(v * rate)
        out[slot, HALF:] = whole(tail)
    if late:
        for at, (k, o) in enumerate(slots(False)):
            out[place(where_ref, k, o)] = refs[0][at]


def place(where_ref, k, o):
    return (where_ref[1] ^ k) * 4 + lax.rem(where_ref[0] + o, 4)


def whole(v):
    return jnp.clip(jnp.round(v), -LEVELS, LEVELS).astype(jnp.int32).astype(jnp.int16)


def decode(coded, quad, extra, message):
    row = lax.broadcasted_iota(jnp.int32, (EXTRA, HALF), 0)

    def one(slot, carry):
        total, rest = carry
        tail = coded[slot, HALF:].astype(jnp.int32).astype(jnp.float32)
        scale = scale_of(tail[1:2]) * (1.0 / LEVELS)
        total = total + coded[slot, :HALF].astype(jnp.int32).astype(jnp.float32) * scale
        rest = rest + jnp.where(row == 0, tail[0:1] * scale, jnp.where(row == 1, tail[2:3], 0.0))
        return total, rest

    start = jnp.zeros((HALF, HALF), jnp.float32), jnp.zeros((EXTRA, HALF), jnp.float32)
    total, extra[...] = lax.fori_loop(0, 16, one, start)
    quad[...] = total
    most = jnp.max(jnp.abs(total), axis=0, keepdims=True)
    code = jnp.ceil(jnp.log2(jnp.maximum(most, 1e-37)) * 256.0)
    message[:HALF] = whole(total * (LEVELS / scale_of(code)))
    message[HALF:] = whole(jnp.broadcast_to(code, (PACK, HALF)))


def opened(message):
    scale = scale_of(message[HALF:].astype(jnp.int32).astype(jnp.float32)[:1]) * (1.0 / LEVELS)
    return message[:HALF].astype(jnp.int32).astype(jnp.float32) * scale


def encoded(late, where, *parts):
    count = 16 if late else len(slots(False))
    return pl.pallas_call(
        functools.partial(encode, late),
        out_shape=jax.ShapeDtypeStruct((count, HALF + PACK, HALF), jnp.int16),
        in_specs=[SMEM] + [VMEM] * len(parts),
        out_specs=VMEM,
        compiler_params=pltpu.CompilerParams(vmem_limit_bytes=8 << 20),
        cost_estimate=pl.CostEstimate(flops=2 << 20, bytes_accessed=3 << 20, transcendentals=0),
        name="encode_late" if late else "encode_early",
    )(where, *parts)


def decoded(coded):
    return pl.pallas_call(
        decode,
        out_shape=(
            jax.ShapeDtypeStruct((HALF, HALF), jnp.float32),
            jax.ShapeDtypeStruct((EXTRA, HALF), jnp.float32),
            jax.ShapeDtypeStruct((HALF + PACK, HALF), jnp.int16),
        ),
        in_specs=[VMEM],
        out_specs=(VMEM, VMEM, VMEM),
        compiler_params=pltpu.CompilerParams(vmem_limit_bytes=8 << 20),
        cost_estimate=pl.CostEstimate(flops=2 << 20, bytes_accessed=1 << 20, transcendentals=0),
        name="decode",
    )(coded)


def assemble(how, quad, extra, r1, r2, out):
    turn1, half1, turn2, diagonal = how[0] == 1, how[1], how[2] == 1, how[3] == 1
    r = lax.broadcasted_iota(jnp.int32, (HALF, HALF), 0)
    c = lax.broadcasted_iota(jnp.int32, (HALF, HALF), 1)
    m, got1, got2 = quad[...], opened(r1), opened(r2)
    turned2 = got2.T
    own = jnp.where(r <= c, m, m.T)
    cross = jnp.where(r > c, m, jnp.where(r == c, extra[0:1], turned2))
    q1 = jnp.where(diagonal, own, jnp.where(turn1, got1.T, got1))
    q2 = jnp.where(diagonal, cross, jnp.where(turn2, turned2, got2))
    total = extra[1:2]
    out[:, :HALF] = jnp.where(half1 == 0, q1, q2) / total
    out[:, HALF:] = jnp.where(half1 == 0, q2, q1) / total


def assembled(how, quad, extra, r1, r2):
    vmem = pl.BlockSpec(memory_space=pltpu.VMEM)
    return pl.pallas_call(
        assemble,
        out_shape=jax.ShapeDtypeStruct((HALF, 2 * HALF), jnp.float32),
        in_specs=[pl.BlockSpec(memory_space=pltpu.SMEM)] + [vmem] * 4,
        out_specs=vmem,
        compiler_params=pltpu.CompilerParams(vmem_limit_bytes=4 << 20),
        cost_estimate=pl.CostEstimate(flops=1 << 20, bytes_accessed=1 << 19, transcendentals=0),
        name="assemble",
    )(how, quad, extra, r1, r2)


def activated(window_of, code, weights, bias):
    v = bias
    for lag in range(weights.shape[0]):
        v = v + jnp.where(code >= lag, weights[lag : lag + 1] * window_of(lag), 0.0)
    return jnp.where(code >= 0, v * (1.0 / (1.0 + jnp.exp(-v))), 0.0)


def codes(group, doc_start, counts):
    token = group * HALF + lax.broadcasted_iota(jnp.int32, (1, HALF), 1)
    place = lax.axis_index(SEQ) * (8 * HALF) + token
    age = jnp.minimum(place - doc_start[group : group + 1, :], 3)
    code = jnp.where(token < counts[0], age, -1).astype(jnp.float32)
    column = jnp.broadcast_to(code, (HALF, HALF)).T
    return jnp.concatenate([column, column], axis=1)


def conv_body(counts, inputs, weights, bias, doc_start, out, lead, x_in, w_in, b_in, d_in, sems):
    moves = [
        pltpu.make_async_copy(src, dst, sems.at[k])
        for k, (src, dst) in enumerate(((inputs, x_in), (weights, w_in), (bias, b_in), (doc_start, d_in)))
    ]
    for move in moves:
        move.start()
    for move in moves:
        move.wait()
    w = w_in[...].astype(jnp.float32)
    b = b_in[...].reshape(1, 2 * HALF).astype(jnp.float32)
    lead[:16] = x_in[:16, :].astype(jnp.float32)
    lead[16:32] = codes(0, d_in, counts)[:16]
    lead[32:36] = w
    lead[36:37] = b
    for group in range(8):
        base = group * HALF
        code = codes(group, d_in, counts)
        if group:
            wide = x_in[base - 16 : base + HALF, :].astype(jnp.float32)
        else:
            wide = jnp.concatenate([jnp.zeros((16, 2 * HALF), jnp.float32), x_in[:HALF, :].astype(jnp.float32)], axis=0)
        value = activated(lambda lag: wide[16 - lag : 16 - lag + HALF], code, w, b)
        out[base : base + HALF, :] = value.astype(jnp.bfloat16)


def head_body(main, lead, prior, own):
    wide = jnp.concatenate([prior[...].astype(jnp.float32), lead[:16]], axis=0)
    value = activated(lambda lag: wide[8 - lag : 24 - lag], lead[16:32], lead[32:36], lead[36:37])
    own[:16, :] = value.astype(jnp.bfloat16)
    own[16:, :] = main[16:, :]


def conv_main(counts, inputs, weights, bias, doc_start):
    fixed = [pltpu.with_memory_space_constraint(v, pltpu.HBM) for v in (inputs, weights, bias, doc_start)]
    return pl.pallas_call(
        conv_body,
        out_shape=(
            jax.ShapeDtypeStruct(inputs.shape, jnp.bfloat16),
            jax.ShapeDtypeStruct((40, inputs.shape[1]), jnp.float32),
        ),
        in_specs=[SMEM] + [pl.BlockSpec(memory_space=pltpu.HBM)] * 4,
        out_specs=(VMEM, VMEM),
        scratch_shapes=[pltpu.VMEM(v.shape, v.dtype) for v in (inputs, weights, bias, doc_start)]
        + [pltpu.SemaphoreType.DMA((4,))],
        compiler_params=pltpu.CompilerParams(vmem_limit_bytes=8 << 20),
        cost_estimate=pl.CostEstimate(flops=8 << 20, bytes_accessed=1 << 20, transcendentals=1 << 19),
        name="conv_main",
    )(counts, *fixed)


def conv_head(main, lead, prior):
    return pl.pallas_call(
        head_body,
        out_shape=jax.ShapeDtypeStruct(main.shape, jnp.bfloat16),
        in_specs=[VMEM] * 3,
        out_specs=VMEM,
        compiler_params=pltpu.CompilerParams(vmem_limit_bytes=8 << 20),
        cost_estimate=pl.CostEstimate(flops=1 << 20, bytes_accessed=1 << 20, transcendentals=0),
        name="conv_head",
    )(main, lead, prior)


def on_device(inputs, conv_weight, conv_bias, doc_start, counts):
    pairs, table = delivery()
    length, _ = inputs.shape
    core, z, x = lax.axis_index(CORE), lax.axis_index(ZL), lax.axis_index(X)
    count = counts[0]

    shards = lax.axis_size(SEQ)
    prior = lax.ppermute(inputs[length - 8 :], SEQ, [(i, i + 1) for i in range(shards - 1)])
    starts = doc_start.reshape(8, HALF)
    main, lead = conv_main(counts, inputs, conv_weight, conv_bias, starts)
    own = conv_head(main, lead, prior)

    ct = lax.ppermute(own, ZL, [(TAU[i], i) for i in range(4)])
    f1 = around(own, X, 1)
    f3 = around(own, X, 3)
    f2 = around(own, X, 2)
    c1 = flipped(own, ZL)

    where = jnp.stack([x, z, core, count]).astype(jnp.int32)
    keep, send = multiplied(False, where, own, f2, ct)
    got = flipped(send, CORE)
    first = encoded(False, where, keep, got)
    keep, send = multiplied(True, where, own, f2, f1, f3, ct, c1)
    coded = encoded(True, where, keep, flipped(send, CORE), first)
    quad, extra, message = decoded(lax.all_to_all(coded, CHIPS, split_axis=0, concat_axis=0, tiled=True))

    r1 = lax.ppermute(message, AXES, pairs[0])
    r2 = lax.ppermute(message, AXES, pairs[1])
    how = lax.dynamic_index_in_dim(jnp.asarray(table), lax.axis_index(AXES), keepdims=False)
    return assembled(how, quad, extra, r1, r2)


def solution(mesh):
    torus = Mesh(mesh.devices.reshape(SIZES), AXES)
    mp = (ZL, X)
    placed = (P(SEQ, mp), P(None, mp), P(mp), P(SEQ), P(SEQ))

    return jax.shard_map(on_device, mesh=torus, in_specs=placed, out_specs=P(SEQ, mp), check_vma=False)
```

profile of v0, /device:TPU:186, one launch (start us, length us, event | category | flops | bytes accessed | tf_op | source)
XLA Modules:
  0.0 107.7 jit_solution(17407953373252445379)
XLA Ops:
  0.7 1.9 %collective-permute-start = (bf16[8,256]{1,0:T(8,128)(2,1)S(1)}, bf16[8,256]{1,0:T(8,128)(2,1)S(1)}, u32[]{:S(2)}, u32[]{:S(2)}) collective-permute-start(bf16[8,256]{1,0:T(8,128)(2,1)S(1)} %slice.3), channel_id=1, source_target_pairs={{0,16},{16,32},{32,48},{48,64},{64,80},{80,96},{96,112},{112,128},... | collective-permute-start | bytes 12296 | tf_op jit(solution)/shard_map/ppermute | solution.py:346
  3.3 2.1 %conv_main.1 = (bf16[1024,256]{1,0:T(8,128)(2,1)S(1)}, f32[40,256]{1,0:T(8,128)S(1)}) custom-call(s32[1]{0:T(128)S(6)} %copy.7.counts, bf16[1024,256]{1,0:T(8,128)(2,1)} %inputs.1, bf16[4,256]{1,0:T(4,128)(2,1)} %weights.1, bf16[256]{0:T(256)(128)(2,1)} %bias.1, s32[8,128]{1,0:T(8,128)} %bitcast.6), custom_call_target="tpu_custom_call" | custom-call | flops 8388608 | bytes 1048576 | tf_op jit(solution)/shard_map/conv_main/pallas_call | solution.py:311
  5.6 4.3 %collective-permute-start.5 = (bf16[1024,256]{1,0:T(8,128)(2,1)S(1)}, bf16[1024,256]{1,0:T(8,128)(2,1)S(1)}, u32[]{:S(2)}, u32[]{:S(2)}) collective-permute-start(bf16[1024,256]{1,0:T(8,128)(2,1)S(1)} %conv_head.1.refs_0_), channel_id=1, source_target_pairs={{0,4},{4,0},{8,12},{12,8},{1,5},{5,1},{9,13},{13,9},{2,6},{6,2},{1... | collective-permute-start | bytes 1572872 | tf_op jit(solution)/shard_map/ppermute | solution.py:87
  9.9 1.9 %collective-permute-start.4 = (bf16[1024,256]{1,0:T(8,128)(2,1)S(1)}, bf16[1024,256]{1,0:T(8,128)(2,1)S(1)}, u32[]{:S(2)}, u32[]{:S(2)}) collective-permute-start(bf16[1024,256]{1,0:T(8,128)(2,1)S(1)} %conv_head.1.refs_0_), channel_id=1, source_target_pairs={{12,0},{8,4},{0,8},{4,12},{13,1},{9,5},{1,9},{5,13},{14,2},{10,6},... | collective-permute-start | bytes 1572872 | tf_op jit(solution)/shard_map/ppermute | solution.py:351
  11.9 3.4 %collective-permute-start.3 = (bf16[1024,256]{1,0:T(8,128)(2,1)S(1)}, bf16[1024,256]{1,0:T(8,128)(2,1)S(1)}, u32[]{:S(2)}, u32[]{:S(2)}) collective-permute-start(bf16[1024,256]{1,0:T(8,128)(2,1)S(1)} %conv_head.1.refs_0_), channel_id=1, source_target_pairs={{3,0},{0,1},{1,2},{2,3},{7,4},{4,5},{5,6},{6,7},{11,8},{8,9},{9,10... | collective-permute-start | bytes 1572872 | tf_op jit(solution)/shard_map/ppermute | solution.py:82
  15.3 2.4 %collective-permute-start.2 = (bf16[1024,256]{1,0:T(8,128)(2,1)S(1)}, bf16[1024,256]{1,0:T(8,128)(2,1)S(1)}, u32[]{:S(2)}, u32[]{:S(2)}) collective-permute-start(bf16[1024,256]{1,0:T(8,128)(2,1)S(1)} %conv_head.1.refs_0_), channel_id=1, source_target_pairs={{1,0},{2,1},{3,2},{0,3},{5,4},{6,5},{7,6},{4,7},{9,8},{10,9},{11,1... | collective-permute-start | bytes 1572872 | tf_op jit(solution)/shard_map/ppermute | solution.py:82
  17.7 4.0 %collective-permute-start.1 = (bf16[1024,256]{1,0:T(8,128)(2,1)S(1)}, bf16[1024,256]{1,0:T(8,128)(2,1)S(1)}, u32[]{:S(2)}, u32[]{:S(2)}) collective-permute-start(bf16[1024,256]{1,0:T(8,128)(2,1)S(1)} %conv_head.1.refs_0_), channel_id=1, source_target_pairs={{2,0},{3,1},{0,2},{1,3},{6,4},{7,5},{4,6},{5,7},{10,8},{11,9},{8,1... | collective-permute-start | bytes 1572872 | tf_op jit(solution)/shard_map/ppermute | solution.py:82
  21.8 3.6 %collective-permute-done.5.refs_5_ = bf16[1024,256]{1,0:T(8,128)(2,1)S(1)} collective-permute-done((bf16[1024,256]{1,0:T(8,128)(2,1)S(1)}, bf16[1024,256]{1,0:T(8,128)(2,1)S(1)}, u32[]{:S(2)}, u32[]{:S(2)}) %collective-permute-start.5) | collective-permute-done | bytes 524320 | tf_op jit(solution)/shard_map/ppermute | solution.py:87
  25.4 1.9 %collective-permute-done.4.refs_4_.refs_2_ = bf16[1024,256]{1,0:T(8,128)(2,1)S(1)} collective-permute-done((bf16[1024,256]{1,0:T(8,128)(2,1)S(1)}, bf16[1024,256]{1,0:T(8,128)(2,1)S(1)}, u32[]{:S(2)}, u32[]{:S(2)}) %collective-permute-start.4) | collective-permute-done | bytes 524320 | tf_op jit(solution)/shard_map/ppermute | solution.py:351
  27.4 0.7 collective-permute-done.2.refs_2_
  28.1 11.9 %collective-permute-done.1.refs_1_ = bf16[1024,256]{1,0:T(8,128)(2,1)S(1)} collective-permute-done((bf16[1024,256]{1,0:T(8,128)(2,1)S(1)}, bf16[1024,256]{1,0:T(8,128)(2,1)S(1)}, u32[]{:S(2)}, u32[]{:S(2)}) %collective-permute-start.1) | collective-permute-done | bytes 524320 | tf_op jit(solution)/shard_map/ppermute | solution.py:82
  39.9 1.8 %products_late.1 = (f32[10,136,128]{2,1,0:T(8,128)S(1)}, f32[10,136,128]{2,1,0:T(8,128)S(1)}) custom-call(s32[4]{0:T(128)S(1)} %pad_add_fusion.where_ref, bf16[1024,256]{1,0:T(8,128)(2,1)S(1)} %conv_head.1.refs_0_, bf16[1024,256]{1,0:T(8,128)(2,1)S(1)} %collective-permute-done.1.refs_1_, bf16[1024,256]{1,0:T(8,128)(2,1)S(1)} %collective-permute-done.2.refs_2_, ...), custom_call_target="tpu_custom_call" | custom-call | flops 1073741824 | bytes 5242880 | tf_op jit(solution)/shard_map/products_late/pallas_call | solution.py:134
  41.8 5.6 %collective-permute-start.6 = (f32[10,136,128]{2,1,0:T(8,128)S(1)}, f32[10,136,128]{2,1,0:T(8,128)S(1)}, u32[]{:S(2)}, u32[]{:S(2)}) collective-permute-start(f32[10,136,128]{2,1,0:T(8,128)S(1)} %get-tuple-element.17), channel_id=1, source_target_pairs={{0,16},{16,0},{1,17},{17,1},{2,18},{18,2},{3,19},{19,3},{4,20},{20... | collective-permute-start | bytes 2088968 | tf_op jit(solution)/shard_map/ppermute | solution.py:87
  47.4 1.3 %products_early.1 = (f32[6,136,128]{2,1,0:T(8,128)S(1)}, f32[6,136,128]{2,1,0:T(8,128)S(1)}) custom-call(s32[4]{0:T(128)S(1)} %pad_add_fusion.where_ref, bf16[1024,256]{1,0:T(8,128)(2,1)S(1)} %conv_head.1.refs_0_, bf16[1024,256]{1,0:T(8,128)(2,1)S(1)} %collective-permute-done.1.refs_1_, bf16[1024,256]{1,0:T(8,128)(2,1)S(1)} %collective-permute-done.4.refs_4_.refs_2_), custom_call_target="tpu_custom_call" | custom-call | flops 536870912 | bytes 5242880 | tf_op jit(solution)/shard_map/products_early/pallas_call | solution.py:134
  48.7 1.9 %collective-permute-start.7 = (f32[6,136,128]{2,1,0:T(8,128)S(1)}, f32[6,136,128]{2,1,0:T(8,128)S(1)}, u32[]{:S(2)}, u32[]{:S(2)}) collective-permute-start(f32[6,136,128]{2,1,0:T(8,128)S(1)} %get-tuple-element.19), channel_id=1, source_target_pairs={{0,16},{16,0},{1,17},{17,1},{2,18},{18,2},{3,19},{19,3},{4,20},{20... | collective-permute-start | bytes 1253384 | tf_op jit(solution)/shard_map/ppermute | solution.py:87
  50.6 1.7 %collective-permute-done.7.got = f32[6,136,128]{2,1,0:T(8,128)S(1)} collective-permute-done((f32[6,136,128]{2,1,0:T(8,128)S(1)}, f32[6,136,128]{2,1,0:T(8,128)S(1)}, u32[]{:S(2)}, u32[]{:S(2)}) %collective-permute-start.7) | collective-permute-done | bytes 417824 | tf_op jit(solution)/shard_map/ppermute | solution.py:87
  53.0 1.6 %encode_late.1 = s16[16,136,128]{2,1,0:T(8,128)(2,1)} custom-call(s32[4]{0:T(128)S(1)} %pad_add_fusion.where_ref, f32[10,136,128]{2,1,0:T(8,128)S(1)} %get-tuple-element.16.keep, f32[10,136,128]{2,1,0:T(8,128)S(1)} %collective-permute-done.6.got, s16[6,136,128]{2,1,0:T(8,128)(2,1)S(1)} %encode_early.1.refs_0_), custom_call_target="tpu_custom_call" | custom-call | flops 2097152 | bytes 3145728 | tf_op jit(solution)/shard_map/encode_late/pallas_call | solution.py:205
  54.6 12.0 %all-to-all-start = ((s16[16,136,128]{2,1,0:T(8,128)(2,1)}), s16[16,136,128]{2,1,0:T(8,128)(2,1)S(1)}, u32[]{:S(2)}, u32[]{:S(2)}) async-start(s16[16,136,128]{2,1,0:T(8,128)(2,1)} %encode_late.1), calls=%async_computation | async-start | bytes 1114112 | tf_op jit(solution)/shard_map/all_to_all | solution.py:363
  66.6 20.0 %all-to-all-done.coded = s16[16,136,128]{2,1,0:T(8,128)(2,1)S(1)} async-done(((s16[16,136,128]{2,1,0:T(8,128)(2,1)}), s16[16,136,128]{2,1,0:T(8,128)(2,1)S(1)}, u32[]{:S(2)}, u32[]{:S(2)}) %all-to-all-start) | async-done | bytes 557088 | tf_op jit(solution)/shard_map/all_to_all | solution.py:363
  87.0 5.7 %collective-permute-start.9 = (s16[136,128]{1,0:T(8,128)(2,1)S(1)}, s16[136,128]{1,0:T(8,128)(2,1)S(1)}, u32[]{:S(2)}, u32[]{:S(2)}) collective-permute-start(s16[136,128]{1,0:T(8,128)(2,1)S(1)} %get-tuple-element.22), channel_id=1, source_target_pairs={{1,48},{2,80},{3,112},{4,4},{5,36},{6,68},{7,100},{8,8},{9,40},{10... | collective-permute-start | bytes 104456 | tf_op jit(solution)/shard_map/ppermute | solution.py:366
  92.8 1.9 %collective-permute-start.8 = (s16[136,128]{1,0:T(8,128)(2,1)S(1)}, s16[136,128]{1,0:T(8,128)(2,1)S(1)}, u32[]{:S(2)}, u32[]{:S(2)}) collective-permute-start(s16[136,128]{1,0:T(8,128)(2,1)S(1)} %get-tuple-element.22), channel_id=1, source_target_pairs={{1,1},{2,2},{3,3},{4,128},{5,129},{6,130},{7,131},{8,256},{9,257},... | collective-permute-start | bytes 104456 | tf_op jit(solution)/shard_map/ppermute | solution.py:365
  94.7 0.7 dynamic-slice_bitcast_fusion.how
  95.9 10.5 %collective-permute-done.8.r1 = s16[136,128]{1,0:T(8,128)(2,1)S(1)} collective-permute-done((s16[136,128]{1,0:T(8,128)(2,1)S(1)}, s16[136,128]{1,0:T(8,128)(2,1)S(1)}, u32[]{:S(2)}, u32[]{:S(2)}) %collective-permute-start.8) | collective-permute-done | bytes 34848 | tf_op jit(solution)/shard_map/ppermute | solution.py:365
  106.4 1.3 %assemble.1 = f32[128,256]{1,0:T(8,128)} custom-call(s32[4]{0:T(128)S(1)} %dynamic-slice_bitcast_fusion.how, f32[128,128]{1,0:T(8,128)S(1)} %get-tuple-element.20.quad, f32[8,128]{1,0:T(8,128)S(1)} %get-tuple-element.21.extra, s16[136,128]{1,0:T(8,128)(2,1)S(1)} %collective-permute-done.8.r1, s16[136,128]{1,0:T(8,128)(2,1)S(1)} %collective-permute-done.9.r2), custom_call_target="tpu_custom_call" | custom-call | flops 1048576 | bytes 524288 | tf_op jit(solution)/shard_map/assemble/pallas_call | solution.py:249
  (9 shorter events, 2.6 us)
Async XLA Ops:
  0.7 4.9 %collective-permute-start = (bf16[8,256]{1,0:T(8,128)(2,1)S(1)}, bf16[8,256]{1,0:T(8,128)(2,1)S(1)}, u32[]{:S(2)}, u32[]{:S(2)}) collective-permute-start(bf16[8,256]{1,0:T(8,128)(2,1)S(1)} %slice.3), channel_id=1, source_target_pairs={{0,16},{16,32},{32,48},{48,64},{64,80},{80,96},{96,112},{112,128},... | collective-permute-start | bytes 12296 | tf_op jit(solution)/shard_map/ppermute | solution.py:346
  5.6 19.8 %collective-permute-start.5 = (bf16[1024,256]{1,0:T(8,128)(2,1)S(1)}, bf16[1024,256]{1,0:T(8,128)(2,1)S(1)}, u32[]{:S(2)}, u32[]{:S(2)}) collective-permute-start(bf16[1024,256]{1,0:T(8,128)(2,1)S(1)} %conv_head.1.refs_0_), channel_id=1, source_target_pairs={{0,4},{4,0},{8,12},{12,8},{1,5},{5,1},{9,13},{13,9},{2,6},{6,2},{1... | collective-permute-start | bytes 1572872 | tf_op jit(solution)/shard_map/ppermute | solution.py:87
  9.9 17.4 %collective-permute-start.4 = (bf16[1024,256]{1,0:T(8,128)(2,1)S(1)}, bf16[1024,256]{1,0:T(8,128)(2,1)S(1)}, u32[]{:S(2)}, u32[]{:S(2)}) collective-permute-start(bf16[1024,256]{1,0:T(8,128)(2,1)S(1)} %conv_head.1.refs_0_), channel_id=1, source_target_pairs={{12,0},{8,4},{0,8},{4,12},{13,1},{9,5},{1,9},{5,13},{14,2},{10,6},... | collective-permute-start | bytes 1572872 | tf_op jit(solution)/shard_map/ppermute | solution.py:351
  11.9 15.5 %collective-permute-start.3 = (bf16[1024,256]{1,0:T(8,128)(2,1)S(1)}, bf16[1024,256]{1,0:T(8,128)(2,1)S(1)}, u32[]{:S(2)}, u32[]{:S(2)}) collective-permute-start(bf16[1024,256]{1,0:T(8,128)(2,1)S(1)} %conv_head.1.refs_0_), channel_id=1, source_target_pairs={{3,0},{0,1},{1,2},{2,3},{7,4},{4,5},{5,6},{6,7},{11,8},{8,9},{9,10... | collective-permute-start | bytes 1572872 | tf_op jit(solution)/shard_map/ppermute | solution.py:82
  15.3 12.8 %collective-permute-start.2 = (bf16[1024,256]{1,0:T(8,128)(2,1)S(1)}, bf16[1024,256]{1,0:T(8,128)(2,1)S(1)}, u32[]{:S(2)}, u32[]{:S(2)}) collective-permute-start(bf16[1024,256]{1,0:T(8,128)(2,1)S(1)} %conv_head.1.refs_0_), channel_id=1, source_target_pairs={{1,0},{2,1},{3,2},{0,3},{5,4},{6,5},{7,6},{4,7},{9,8},{10,9},{11,1... | collective-permute-start | bytes 1572872 | tf_op jit(solution)/shard_map/ppermute | solution.py:82
  17.7 22.2 %collective-permute-start.1 = (bf16[1024,256]{1,0:T(8,128)(2,1)S(1)}, bf16[1024,256]{1,0:T(8,128)(2,1)S(1)}, u32[]{:S(2)}, u32[]{:S(2)}) collective-permute-start(bf16[1024,256]{1,0:T(8,128)(2,1)S(1)} %conv_head.1.refs_0_), channel_id=1, source_target_pairs={{2,0},{3,1},{0,2},{1,3},{6,4},{7,5},{4,6},{5,7},{10,8},{11,9},{8,1... | collective-permute-start | bytes 1572872 | tf_op jit(solution)/shard_map/ppermute | solution.py:82
  41.8 11.3 %collective-permute-start.6 = (f32[10,136,128]{2,1,0:T(8,128)S(1)}, f32[10,136,128]{2,1,0:T(8,128)S(1)}, u32[]{:S(2)}, u32[]{:S(2)}) collective-permute-start(f32[10,136,128]{2,1,0:T(8,128)S(1)} %get-tuple-element.17), channel_id=1, source_target_pairs={{0,16},{16,0},{1,17},{17,1},{2,18},{18,2},{3,19},{19,3},{4,20},{20... | collective-permute-start | bytes 2088968 | tf_op jit(solution)/shard_map/ppermute | solution.py:87
  48.7 3.7 %collective-permute-start.7 = (f32[6,136,128]{2,1,0:T(8,128)S(1)}, f32[6,136,128]{2,1,0:T(8,128)S(1)}, u32[]{:S(2)}, u32[]{:S(2)}) collective-permute-start(f32[6,136,128]{2,1,0:T(8,128)S(1)} %get-tuple-element.19), channel_id=1, source_target_pairs={{0,16},{16,0},{1,17},{17,1},{2,18},{18,2},{3,19},{19,3},{4,20},{20... | collective-permute-start | bytes 1253384 | tf_op jit(solution)/shard_map/ppermute | solution.py:87
  54.6 32.0 %all-to-all-start = ((s16[16,136,128]{2,1,0:T(8,128)(2,1)}), s16[16,136,128]{2,1,0:T(8,128)(2,1)S(1)}, u32[]{:S(2)}, u32[]{:S(2)}) async-start(s16[16,136,128]{2,1,0:T(8,128)(2,1)} %encode_late.1), calls=%async_computation | async-start | bytes 1114112 | tf_op jit(solution)/shard_map/all_to_all | solution.py:363
  87.0 8.8 %collective-permute-start.9 = (s16[136,128]{1,0:T(8,128)(2,1)S(1)}, s16[136,128]{1,0:T(8,128)(2,1)S(1)}, u32[]{:S(2)}, u32[]{:S(2)}) collective-permute-start(s16[136,128]{1,0:T(8,128)(2,1)S(1)} %get-tuple-element.22), channel_id=1, source_target_pairs={{1,48},{2,80},{3,112},{4,4},{5,36},{6,68},{7,100},{8,8},{9,40},{10... | collective-permute-start | bytes 104456 | tf_op jit(solution)/shard_map/ppermute | solution.py:366
  92.8 13.6 %collective-permute-start.8 = (s16[136,128]{1,0:T(8,128)(2,1)S(1)}, s16[136,128]{1,0:T(8,128)(2,1)S(1)}, u32[]{:S(2)}, u32[]{:S(2)}) collective-permute-start(s16[136,128]{1,0:T(8,128)(2,1)S(1)} %get-tuple-element.22), channel_id=1, source_target_pairs={{1,1},{2,2},{3,3},{4,128},{5,129},{6,130},{7,131},{8,256},{9,257},... | collective-permute-start | bytes 104456 | tf_op jit(solution)/shard_map/ppermute | solution.py:365
where the time goes:
time: 108 us
  waiting for transfers between devices  51.1 us (47%)
  starting transfers between devices  45.2 us (42%)
  Pallas kernels  9.28 us (9%)
  local copies, waits for them, and re-layouts  1.39 us (1%)
    all_to_all x1, waiting for transfers between devices, on_device(): lax.all_to_all(coded, CHIPS, split_axis=0, concat_axis=0, tiled=True)  20 us
    ppermute x3, waiting for transfers between devices, around(): return lax.ppermute(x, axis, [((i + by) % n, i) for i in range(n)])  12.6 us
    all_to_all x1, starting transfers between devices, on_device(): lax.all_to_all(coded, CHIPS, split_axis=0, concat_axis=0, tiled=True)  12 us
    ppermute x3, starting transfers between devices, flipped(): return lax.ppermute(x, axis, [(i, i ^ bit) for i in range(n)])  11.8 us
    ppermute x1, waiting for transfers between devices, on_device(): r1 = lax.ppermute(message, AXES, pairs[0])  10.5 us
    ppermute x3, starting transfers between devices, around(): return lax.ppermute(x, axis, [((i + by) % n, i) for i in range(n)])  9.88 us
    ppermute x1, starting transfers between devices, on_device(): r2 = lax.ppermute(message, AXES, pairs[1])  5.7 us
    ppermute x3, waiting for transfers between devices, flipped(): return lax.ppermute(x, axis, [(i, i ^ bit) for i in range(n)])  5.31 us
  transfers between devices with their start and end apart: 11, of which 9 were waited for; matrix products, arithmetic and copies ran while one was open for 1% of the time, Pallas kernels for 4%

commit v1 on v0

--- a/solution.py
+++ b/solution.py
@@ -15,6 +15,8 @@
 SEQ = (ZH, YW, YA, CORE)
 CHIPS = (ZH, YW, YA)
 TAU = (3, 2, 0, 1)
+HOMES = tuple(tuple(4 * (mp // 4 ^ k) + a for k in range(4) for a in range(4)) for mp in range(16))
+NEAR_FIRST = False
 EARLY = ((0, "own"), (0, "far"), (2, "own"), (2, "far"))
 LATE = ((1, "own"), (1, "far"), (1, "near"), (3, "own"), (3, "far"), (3, "near"), (0, "near"), (2, "near"))
 HALF = 128
@@ -25,50 +27,58 @@
 SMEM = pl.BlockSpec(memory_space=pltpu.SMEM)
 
 
+def number(chip, core, mp):
+    return (chip * 2 + core) * 16 + mp
+
+
+def hops(p, q):
+    def coordinates(device):
+        seq, mp = divmod(device, 16)
+        return mp % 4, seq // 2 % 8, seq // 16 * 4 + mp // 4
+
+    return sum(min((i - j) % n, (j - i) % n) for i, j, n in zip(coordinates(p), coordinates(q), (4, 8, 8)))
+
+
 def delivery():
-    def number(seq_chip, core, mp):
-        return (seq_chip * 2 + core) * 16 + mp
-
     edges = []
-    for seq_chip in range(16):
-        for h in range(2):
-            for mp in range(16):
-                zeta, a = divmod(seq_chip, 4)
-                z, x = divmod(mp, 4)
-                row = 4 * z + a
-                if zeta == z:
-                    col, hc = 4 * z + x, (h if a >= x else 1 - h)
-                elif zeta == z ^ 1:
-                    col, hc = 4 * (z ^ 1) + x, (h if z % 2 else 1 - h)
-                else:
-                    col, hc = 4 * TAU[z] + x, (0 if zeta == z ^ 2 else 1)
-                src = number(seq_chip, h, mp)
-                if row == col:
-                    continue
+    for mp, homes in enumerate(HOMES):
+        z, x = divmod(mp, 4)
+        for content, chip in enumerate(homes):
+            kind, a = divmod(content, 4)
+            row, col = 4 * z + a, 4 * (z, z ^ 1, TAU[z], TAU[z])[kind] + x
+            if row == col:
+                continue
+            for h in range(2):
+                same = (a >= x, z % 2 == 1, h == 0, h == 1)[kind]
+                hc = h if same else 1 - h
+                src = number(chip, h, mp)
                 edges.append((src, number(row, h, col), hc, 0))
                 edges.append((src, number(col, hc, row), h, 1))
-    by_src, by_dst = {}, {}
-    for e, (s, d, _, _) in enumerate(edges):
-        by_src.setdefault(s, []).append(e)
+    by_dst = {}
+    for e, (_, d, _, _) in enumerate(edges):
         by_dst.setdefault(d, []).append(e)
-    colour = {}
-    for first in range(len(edges)):
-        e = first
-        while e not in colour:
-            colour[e] = 0
-            s = edges[e][0]
-            other = [k for k in by_src[s] if k != e][0]
-            colour[other] = 1
-            d = edges[other][1]
-            e = [k for k in by_dst[d] if k != other][0]
-    pairs = ([], [])
+    seen, rounds = set(), ([], [])
+    for start in range(0, len(edges), 2):
+        if start in seen:
+            continue
+        cycle, e = ([], []), start
+        while e not in seen:
+            seen.update((e, e ^ 1))
+            cycle[0].append(e)
+            cycle[1].append(e ^ 1)
+            e = sum(by_dst[edges[e ^ 1][1]]) - (e ^ 1)
+        weight = [sum(2.0 ** hops(*edges[k][:2]) for k in part) for part in cycle]
+        first = 0 if (weight[0] <= weight[1]) == NEAR_FIRST else 1
+        rounds[1].extend(cycle[first])
+        rounds[0].extend(cycle[1 - first])
     table = np.zeros((512, 4), np.int32)
-    for e, (s, d, half, turned) in enumerate(edges):
-        k = colour[e]
-        pairs[k].append((s, d))
-        table[d, 2 * k] = turned
-        if k == 0:
-            table[d, 1] = half
+    for k in range(2):
+        for e in rounds[k]:
+            _, d, half, turned = edges[e]
+            table[d, 2 * k] = turned
+            if k == 0:
+                table[d, 1] = half
+    pairs = tuple([edges[e][:2] for e in part] for part in rounds)
     for mp in range(16):
         for h in range(2):
             own, other = number(mp, h, mp), number(mp, 1 - h, mp)
@@ -168,7 +178,7 @@
 
 
 def place(where_ref, k, o):
-    return (where_ref[1] ^ k) * 4 + lax.rem(where_ref[0] + o, 4)
+    return where_ref[4 + 4 * k + lax.rem(where_ref[0] + o, 4)]
 
 
 def whole(v):
@@ -354,7 +364,8 @@
     f2 = around(own, X, 2)
     c1 = flipped(own, ZL)
 
-    where = jnp.stack([x, z, core, count]).astype(jnp.int32)
+    homes = lax.dynamic_index_in_dim(jnp.asarray(HOMES, jnp.int32), 4 * z + x, keepdims=False)
+    where = jnp.concatenate([jnp.stack([x, z, core, count]).astype(jnp.int32), homes])
     keep, send = multiplied(False, where, own, f2, ct)
     got = flipped(send, CORE)
     first = encoded(False, where, keep, got)
@@ -362,8 +373,8 @@
     coded = encoded(True, where, keep, flipped(send, CORE), first)
     quad, extra, message = decoded(lax.all_to_all(coded, CHIPS, split_axis=0, concat_axis=0, tiled=True))
 
+    r2 = lax.ppermute(message, AXES, pairs[1])
     r1 = lax.ppermute(message, AXES, pairs[0])
-    r2 = lax.ppermute(message, AXES, pairs[1])
     how = lax.dynamic_index_in_dim(jnp.asarray(table), lax.axis_index(AXES), keepdims=False)
     return assembled(how, quad, extra, r1, r2)
 

time: 108 us -> 106 us (0.981)
  the two profiles are of different devices: /device:TPU:186 before, /device:TPU:70 now
where the time goes in v1:
time: 106 us
  waiting for transfers between devices  48.6 us (46%)
  starting transfers between devices  45 us (42%)
  Pallas kernels  9.33 us (9%)
  local copies, waits for them, and re-layouts  2.17 us (2%)
    all_to_all x1, waiting for transfers between devices, on_device(): lax.all_to_all(coded, CHIPS, split_axis=0, concat_axis=0, tiled=True)  20.5 us
    ppermute x1, waiting for transfers between devices, on_device(): ct = lax.ppermute(own, ZL, [(TAU[i], i) for i in range(4)])  13.8 us
    all_to_all x1, starting transfers between devices, on_device(): lax.all_to_all(coded, CHIPS, split_axis=0, concat_axis=0, tiled=True)  12.3 us
    ppermute x3, starting transfers between devices, around(): return lax.ppermute(x, axis, [((i + by) % n, i) for i in range(n)])  9.16 us
    ppermute x3, waiting for transfers between devices, around(): return lax.ppermute(x, axis, [((i + by) % n, i) for i in range(n)])  8.13 us
    ppermute x3, starting transfers between devices, flipped(): return lax.ppermute(x, axis, [(i, i ^ bit) for i in range(n)])  6.25 us
    ppermute x1, starting transfers between devices, on_device(): ct = lax.ppermute(own, ZL, [(TAU[i], i) for i in range(4)])  6.09 us
    ppermute x1, starting transfers between devices, on_device(): r2 = lax.ppermute(message, AXES, pairs[1])  5.26 us
  transfers between devices with their start and end apart: 11, of which 6 were waited for; matrix products, arithmetic and copies ran while one was open for 1% of the time, Pallas kernels for 4%

profile of v1, /device:TPU:70, one launch (start us, length us, event | category | flops | bytes accessed | tf_op | source)
XLA Modules:
  0.0 105.9 jit_solution(5727260164856656174)
XLA Ops:
  0.0 0.7 slice.3
  0.7 1.7 %collective-permute-start = (bf16[8,256]{1,0:T(8,128)(2,1)S(1)}, bf16[8,256]{1,0:T(8,128)(2,1)S(1)}, u32[]{:S(2)}, u32[]{:S(2)}) collective-permute-start(bf16[8,256]{1,0:T(8,128)(2,1)S(1)} %slice.3), channel_id=1, source_target_pairs={{0,16},{16,32},{32,48},{48,64},{64,80},{80,96},{96,112},{112,128},... | collective-permute-start | bytes 12296 | tf_op jit(solution)/shard_map/ppermute | solution.py:356
  3.1 2.1 %conv_main.1 = (bf16[1024,256]{1,0:T(8,128)(2,1)S(1)}, f32[40,256]{1,0:T(8,128)S(1)}) custom-call(s32[1]{0:T(128)S(6)} %copy.8.counts, bf16[1024,256]{1,0:T(8,128)(2,1)} %inputs.1, bf16[4,256]{1,0:T(4,128)(2,1)} %weights.1, bf16[256]{0:T(256)(128)(2,1)} %bias.1, s32[8,128]{1,0:T(8,128)} %bitcast.8), custom_call_target="tpu_custom_call" | custom-call | flops 8388608 | bytes 1048576 | tf_op jit(solution)/shard_map/conv_main/pallas_call | solution.py:321
  5.3 1.9 %collective-permute-start.5 = (bf16[1024,256]{1,0:T(8,128)(2,1)S(1)}, bf16[1024,256]{1,0:T(8,128)(2,1)S(1)}, u32[]{:S(2)}, u32[]{:S(2)}) collective-permute-start(bf16[1024,256]{1,0:T(8,128)(2,1)S(1)} %conv_head.1.refs_0_), channel_id=1, source_target_pairs={{0,4},{4,0},{8,12},{12,8},{1,5},{5,1},{9,13},{13,9},{2,6},{6,2},{1... | collective-permute-start | bytes 1572872 | tf_op jit(solution)/shard_map/ppermute | solution.py:97
  7.2 6.1 %collective-permute-start.4 = (bf16[1024,256]{1,0:T(8,128)(2,1)S(1)}, bf16[1024,256]{1,0:T(8,128)(2,1)S(1)}, u32[]{:S(2)}, u32[]{:S(2)}) collective-permute-start(bf16[1024,256]{1,0:T(8,128)(2,1)S(1)} %conv_head.1.refs_0_), channel_id=1, source_target_pairs={{12,0},{8,4},{0,8},{4,12},{13,1},{9,5},{1,9},{5,13},{14,2},{10,6},... | collective-permute-start | bytes 1572872 | tf_op jit(solution)/shard_map/ppermute | solution.py:361
  13.3 2.8 %collective-permute-start.3 = (bf16[1024,256]{1,0:T(8,128)(2,1)S(1)}, bf16[1024,256]{1,0:T(8,128)(2,1)S(1)}, u32[]{:S(2)}, u32[]{:S(2)}) collective-permute-start(bf16[1024,256]{1,0:T(8,128)(2,1)S(1)} %conv_head.1.refs_0_), channel_id=1, source_target_pairs={{3,0},{0,1},{1,2},{2,3},{7,4},{4,5},{5,6},{6,7},{11,8},{8,9},{9,10... | collective-permute-start | bytes 1572872 | tf_op jit(solution)/shard_map/ppermute | solution.py:92
  16.1 3.1 %collective-permute-start.2 = (bf16[1024,256]{1,0:T(8,128)(2,1)S(1)}, bf16[1024,256]{1,0:T(8,128)(2,1)S(1)}, u32[]{:S(2)}, u32[]{:S(2)}) collective-permute-start(bf16[1024,256]{1,0:T(8,128)(2,1)S(1)} %conv_head.1.refs_0_), channel_id=1, source_target_pairs={{1,0},{2,1},{3,2},{0,3},{5,4},{6,5},{7,6},{4,7},{9,8},{10,9},{11,1... | collective-permute-start | bytes 1572872 | tf_op jit(solution)/shard_map/ppermute | solution.py:92
  19.2 3.3 %collective-permute-start.1 = (bf16[1024,256]{1,0:T(8,128)(2,1)S(1)}, bf16[1024,256]{1,0:T(8,128)(2,1)S(1)}, u32[]{:S(2)}, u32[]{:S(2)}) collective-permute-start(bf16[1024,256]{1,0:T(8,128)(2,1)S(1)} %conv_head.1.refs_0_), channel_id=1, source_target_pairs={{2,0},{3,1},{0,2},{1,3},{6,4},{7,5},{4,6},{5,7},{10,8},{11,9},{8,1... | collective-permute-start | bytes 1572872 | tf_op jit(solution)/shard_map/ppermute | solution.py:92
  22.5 0.7 dynamic-slice_bitcast_fusion
  23.3 13.8 %collective-permute-done.4.refs_4_.refs_2_ = bf16[1024,256]{1,0:T(8,128)(2,1)S(1)} collective-permute-done((bf16[1024,256]{1,0:T(8,128)(2,1)S(1)}, bf16[1024,256]{1,0:T(8,128)(2,1)S(1)}, u32[]{:S(2)}, u32[]{:S(2)}) %collective-permute-start.4) | collective-permute-done | bytes 524320 | tf_op jit(solution)/shard_map/ppermute | solution.py:361
  37.0 8.1 %collective-permute-done.2.refs_2_ = bf16[1024,256]{1,0:T(8,128)(2,1)S(1)} collective-permute-done((bf16[1024,256]{1,0:T(8,128)(2,1)S(1)}, bf16[1024,256]{1,0:T(8,128)(2,1)S(1)}, u32[]{:S(2)}, u32[]{:S(2)}) %collective-permute-start.2) | collective-permute-done | bytes 524320 | tf_op jit(solution)/shard_map/ppermute | solution.py:92
  45.2 1.9 %products_late.1 = (f32[10,136,128]{2,1,0:T(8,128)S(1)}, f32[10,136,128]{2,1,0:T(8,128)S(1)}) custom-call(s32[20]{0:T(128)S(1)} %concatenate.3.where_ref, bf16[1024,256]{1,0:T(8,128)(2,1)S(1)} %conv_head.1.refs_0_, bf16[1024,256]{1,0:T(8,128)(2,1)S(1)} %collective-permute-done.1.refs_1_, bf16[1024,256]{1,0:T(8,128)(2,1)S(1)} %collective-permute-done.2.refs_2_, ...), custom_call_target="tpu_custom_call" | custom-call | flops 1073741824 | bytes 5242880 | tf_op jit(solution)/shard_map/products_late/pallas_call | solution.py:144
  47.1 2.0 %collective-permute-start.6 = (f32[10,136,128]{2,1,0:T(8,128)S(1)}, f32[10,136,128]{2,1,0:T(8,128)S(1)}, u32[]{:S(2)}, u32[]{:S(2)}) collective-permute-start(f32[10,136,128]{2,1,0:T(8,128)S(1)} %get-tuple-element.17), channel_id=1, source_target_pairs={{0,16},{16,0},{1,17},{17,1},{2,18},{18,2},{3,19},{19,3},{4,20},{20... | collective-permute-start | bytes 2088968 | tf_op jit(solution)/shard_map/ppermute | solution.py:97
  49.0 1.3 %products_early.1 = (f32[6,136,128]{2,1,0:T(8,128)S(1)}, f32[6,136,128]{2,1,0:T(8,128)S(1)}) custom-call(s32[20]{0:T(128)S(1)} %concatenate.3.where_ref, bf16[1024,256]{1,0:T(8,128)(2,1)S(1)} %conv_head.1.refs_0_, bf16[1024,256]{1,0:T(8,128)(2,1)S(1)} %collective-permute-done.1.refs_1_, bf16[1024,256]{1,0:T(8,128)(2,1)S(1)} %collective-permute-done.4.refs_4_.refs_2_), custom_call_target="tpu_custom_call" | custom-call | flops 536870912 | bytes 5242880 | tf_op jit(solution)/shard_map/products_early/pallas_call | solution.py:144
  50.3 2.4 %collective-permute-start.7 = (f32[6,136,128]{2,1,0:T(8,128)S(1)}, f32[6,136,128]{2,1,0:T(8,128)S(1)}, u32[]{:S(2)}, u32[]{:S(2)}) collective-permute-start(f32[6,136,128]{2,1,0:T(8,128)S(1)} %get-tuple-element.19), channel_id=1, source_target_pairs={{0,16},{16,0},{1,17},{17,1},{2,18},{18,2},{3,19},{19,3},{4,20},{20... | collective-permute-start | bytes 1253384 | tf_op jit(solution)/shard_map/ppermute | solution.py:97
  52.7 1.4 %collective-permute-done.7.got = f32[6,136,128]{2,1,0:T(8,128)S(1)} collective-permute-done((f32[6,136,128]{2,1,0:T(8,128)S(1)}, f32[6,136,128]{2,1,0:T(8,128)S(1)}, u32[]{:S(2)}, u32[]{:S(2)}) %collective-permute-start.7) | collective-permute-done | bytes 417824 | tf_op jit(solution)/shard_map/ppermute | solution.py:97
  54.7 1.6 %encode_late.1 = s16[16,136,128]{2,1,0:T(8,128)(2,1)} custom-call(s32[20]{0:T(128)S(1)} %concatenate.3.where_ref, f32[10,136,128]{2,1,0:T(8,128)S(1)} %get-tuple-element.16.keep, f32[10,136,128]{2,1,0:T(8,128)S(1)} %collective-permute-done.6.got, s16[6,136,128]{2,1,0:T(8,128)(2,1)S(1)} %encode_early.1.refs_0_), custom_call_target="tpu_custom_call" | custom-call | flops 2097152 | bytes 3145728 | tf_op jit(solution)/shard_map/encode_late/pallas_call | solution.py:215
  56.3 12.3 %all-to-all-start = ((s16[16,136,128]{2,1,0:T(8,128)(2,1)}), s16[16,136,128]{2,1,0:T(8,128)(2,1)S(1)}, u32[]{:S(2)}, u32[]{:S(2)}) async-start(s16[16,136,128]{2,1,0:T(8,128)(2,1)} %encode_late.1), calls=%async_computation | async-start | bytes 1114112 | tf_op jit(solution)/shard_map/all_to_all | solution.py:374
  68.6 20.5 %all-to-all-done.coded = s16[16,136,128]{2,1,0:T(8,128)(2,1)S(1)} async-done(((s16[16,136,128]{2,1,0:T(8,128)(2,1)}), s16[16,136,128]{2,1,0:T(8,128)(2,1)S(1)}, u32[]{:S(2)}, u32[]{:S(2)}) %all-to-all-start) | async-done | bytes 557088 | tf_op jit(solution)/shard_map/all_to_all | solution.py:374
  89.6 5.3 %collective-permute-start.9 = (s16[136,128]{1,0:T(8,128)(2,1)S(1)}, s16[136,128]{1,0:T(8,128)(2,1)S(1)}, u32[]{:S(2)}, u32[]{:S(2)}) collective-permute-start(s16[136,128]{1,0:T(8,128)(2,1)S(1)} %get-tuple-element.22), channel_id=1, source_target_pairs={{32,1},{1,48},{48,17},{17,32},{64,2},{2,80},{80,18},{18,64},{96,3}... | collective-permute-start | bytes 104456 | tf_op jit(solution)/shard_map/ppermute | solution.py:376
  94.8 4.2 %collective-permute-start.8 = (s16[136,128]{1,0:T(8,128)(2,1)S(1)}, s16[136,128]{1,0:T(8,128)(2,1)S(1)}, u32[]{:S(2)}, u32[]{:S(2)}) collective-permute-start(s16[136,128]{1,0:T(8,128)(2,1)S(1)} %get-tuple-element.22), channel_id=1, source_target_pairs={{32,32},{1,1},{48,48},{17,17},{64,64},{2,2},{80,80},{18,18},{96,96... | collective-permute-start | bytes 104456 | tf_op jit(solution)/shard_map/ppermute | solution.py:377
  99.0 0.7 dynamic-slice_bitcast_fusion.1.how
  100.3 4.3 %collective-permute-done.8.r1 = s16[136,128]{1,0:T(8,128)(2,1)S(1)} collective-permute-done((s16[136,128]{1,0:T(8,128)(2,1)S(1)}, s16[136,128]{1,0:T(8,128)(2,1)S(1)}, u32[]{:S(2)}, u32[]{:S(2)}) %collective-permute-start.8) | collective-permute-done | bytes 34848 | tf_op jit(solution)/shard_map/ppermute | solution.py:377
  104.6 1.3 %assemble.1 = f32[128,256]{1,0:T(8,128)} custom-call(s32[4]{0:T(128)S(1)} %dynamic-slice_bitcast_fusion.1.how, f32[128,128]{1,0:T(8,128)S(1)} %get-tuple-element.20.quad, f32[8,128]{1,0:T(8,128)S(1)} %get-tuple-element.21.extra, s16[136,128]{1,0:T(8,128)(2,1)S(1)} %collective-permute-done.8.r1, s16[136,128]{1,0:T(8,128)(2,1)S(1)} %collective-permute-done.9.r2), custom_call_target="tpu_custom_call" | custom-call | flops 1048576 | bytes 524288 | tf_op jit(solution)/shard_map/assemble/pallas_call | solution.py:259
  (10 shorter events, 1.8 us)
Async XLA Ops:
  0.7 4.5 %collective-permute-start = (bf16[8,256]{1,0:T(8,128)(2,1)S(1)}, bf16[8,256]{1,0:T(8,128)(2,1)S(1)}, u32[]{:S(2)}, u32[]{:S(2)}) collective-permute-start(bf16[8,256]{1,0:T(8,128)(2,1)S(1)} %slice.3), channel_id=1, source_target_pairs={{0,16},{16,32},{32,48},{48,64},{64,80},{80,96},{96,112},{112,128},... | collective-permute-start | bytes 12296 | tf_op jit(solution)/shard_map/ppermute | solution.py:356
  5.3 18.0 %collective-permute-start.5 = (bf16[1024,256]{1,0:T(8,128)(2,1)S(1)}, bf16[1024,256]{1,0:T(8,128)(2,1)S(1)}, u32[]{:S(2)}, u32[]{:S(2)}) collective-permute-start(bf16[1024,256]{1,0:T(8,128)(2,1)S(1)} %conv_head.1.refs_0_), channel_id=1, source_target_pairs={{0,4},{4,0},{8,12},{12,8},{1,5},{5,1},{9,13},{13,9},{2,6},{6,2},{1... | collective-permute-start | bytes 1572872 | tf_op jit(solution)/shard_map/ppermute | solution.py:97
  7.2 29.8 %collective-permute-start.4 = (bf16[1024,256]{1,0:T(8,128)(2,1)S(1)}, bf16[1024,256]{1,0:T(8,128)(2,1)S(1)}, u32[]{:S(2)}, u32[]{:S(2)}) collective-permute-start(bf16[1024,256]{1,0:T(8,128)(2,1)S(1)} %conv_head.1.refs_0_), channel_id=1, source_target_pairs={{12,0},{8,4},{0,8},{4,12},{13,1},{9,5},{1,9},{5,13},{14,2},{10,6},... | collective-permute-start | bytes 1572872 | tf_op jit(solution)/shard_map/ppermute | solution.py:361
  13.3 23.7 %collective-permute-start.3 = (bf16[1024,256]{1,0:T(8,128)(2,1)S(1)}, bf16[1024,256]{1,0:T(8,128)(2,1)S(1)}, u32[]{:S(2)}, u32[]{:S(2)}) collective-permute-start(bf16[1024,256]{1,0:T(8,128)(2,1)S(1)} %conv_head.1.refs_0_), channel_id=1, source_target_pairs={{3,0},{0,1},{1,2},{2,3},{7,4},{4,5},{5,6},{6,7},{11,8},{8,9},{9,10... | collective-permute-start | bytes 1572872 | tf_op jit(solution)/shard_map/ppermute | solution.py:92
  16.1 29.1 %collective-permute-start.2 = (bf16[1024,256]{1,0:T(8,128)(2,1)S(1)}, bf16[1024,256]{1,0:T(8,128)(2,1)S(1)}, u32[]{:S(2)}, u32[]{:S(2)}) collective-permute-start(bf16[1024,256]{1,0:T(8,128)(2,1)S(1)} %conv_head.1.refs_0_), channel_id=1, source_target_pairs={{1,0},{2,1},{3,2},{0,3},{5,4},{6,5},{7,6},{4,7},{9,8},{10,9},{11,1... | collective-permute-start | bytes 1572872 | tf_op jit(solution)/shard_map/ppermute | solution.py:92
  19.2 26.0 %collective-permute-start.1 = (bf16[1024,256]{1,0:T(8,128)(2,1)S(1)}, bf16[1024,256]{1,0:T(8,128)(2,1)S(1)}, u32[]{:S(2)}, u32[]{:S(2)}) collective-permute-start(bf16[1024,256]{1,0:T(8,128)(2,1)S(1)} %conv_head.1.refs_0_), channel_id=1, source_target_pairs={{2,0},{3,1},{0,2},{1,3},{6,4},{7,5},{4,6},{5,7},{10,8},{11,9},{8,1... | collective-permute-start | bytes 1572872 | tf_op jit(solution)/shard_map/ppermute | solution.py:92
  47.1 7.7 %collective-permute-start.6 = (f32[10,136,128]{2,1,0:T(8,128)S(1)}, f32[10,136,128]{2,1,0:T(8,128)S(1)}, u32[]{:S(2)}, u32[]{:S(2)}) collective-permute-start(f32[10,136,128]{2,1,0:T(8,128)S(1)} %get-tuple-element.17), channel_id=1, source_target_pairs={{0,16},{16,0},{1,17},{17,1},{2,18},{18,2},{3,19},{19,3},{4,20},{20... | collective-permute-start | bytes 2088968 | tf_op jit(solution)/shard_map/ppermute | solution.py:97
  50.3 3.7 %collective-permute-start.7 = (f32[6,136,128]{2,1,0:T(8,128)S(1)}, f32[6,136,128]{2,1,0:T(8,128)S(1)}, u32[]{:S(2)}, u32[]{:S(2)}) collective-permute-start(f32[6,136,128]{2,1,0:T(8,128)S(1)} %get-tuple-element.19), channel_id=1, source_target_pairs={{0,16},{16,0},{1,17},{17,1},{2,18},{18,2},{3,19},{19,3},{4,20},{20... | collective-permute-start | bytes 1253384 | tf_op jit(solution)/shard_map/ppermute | solution.py:97
  56.3 32.8 %all-to-all-start = ((s16[16,136,128]{2,1,0:T(8,128)(2,1)}), s16[16,136,128]{2,1,0:T(8,128)(2,1)S(1)}, u32[]{:S(2)}, u32[]{:S(2)}) async-start(s16[16,136,128]{2,1,0:T(8,128)(2,1)} %encode_late.1), calls=%async_computation | async-start | bytes 1114112 | tf_op jit(solution)/shard_map/all_to_all | solution.py:374
  89.6 10.7 %collective-permute-start.9 = (s16[136,128]{1,0:T(8,128)(2,1)S(1)}, s16[136,128]{1,0:T(8,128)(2,1)S(1)}, u32[]{:S(2)}, u32[]{:S(2)}) collective-permute-start(s16[136,128]{1,0:T(8,128)(2,1)S(1)} %get-tuple-element.22), channel_id=1, source_target_pairs={{32,1},{1,48},{48,17},{17,32},{64,2},{2,80},{80,18},{18,64},{96,3}... | collective-permute-start | bytes 104456 | tf_op jit(solution)/shard_map/ppermute | solution.py:376
  94.8 9.7 %collective-permute-start.8 = (s16[136,128]{1,0:T(8,128)(2,1)S(1)}, s16[136,128]{1,0:T(8,128)(2,1)S(1)}, u32[]{:S(2)}, u32[]{:S(2)}) collective-permute-start(s16[136,128]{1,0:T(8,128)(2,1)S(1)} %get-tuple-element.22), channel_id=1, source_target_pairs={{32,32},{1,1},{48,48},{17,17},{64,64},{2,2},{80,80},{18,18},{96,96... | collective-permute-start | bytes 104456 | tf_op jit(solution)/shard_map/ppermute | solution.py:377
